TPU v7x, 256 devices: a whole 4x4x8 slice. The times are simulated.
256 devices in a mesh: dp: 64 (over z, y, core), cp: 4 (over x).
Axes of the slice: x: 4, y: 4, z: 8, core: 2. Of those that a mesh axis runs over, the one named last changes fastest.
Arguments:
- x_in: bfloat16 [128, 2048, 640], P('dp', 'cp')
- grad_y: bfloat16 [128, 2048, 640], P('dp', 'cp')
- ln_gamma: float32 [640], replicated
- ln_beta: float32 [640], replicated
- w_q: bfloat16 [640, 8, 80], replicated
- w_k: bfloat16 [640, 8, 80], replicated
- w_v: bfloat16 [640, 8, 80], replicated
- w_o: bfloat16 [8, 80, 640], replicated
- b_o: float32 [640], replicated
Outputs:
- output 1: bfloat16 [128, 2048, 640], P('dp', 'cp')
- output 2: bfloat16 [128, 2048, 640], P('dp', 'cp')
- output 3: float32 [640], replicated
- output 4: float32 [640], replicated
- output 5: float32 [640, 8, 80], replicated
- output 6: float32 [640, 8, 80], replicated
- output 7: float32 [640, 8, 80], replicated
- output 8: float32 [8, 80, 640], replicated
- output 9: float32 [640], replicated
All inputs are finite; a program needn't handle non-finite values.
Results may differ from a plain program's by a relative error of at most 0.0149178.
Values are sent between devices in bfloat16 or wider.
A program may use at most 768 MiB of HBM per device.

v0:
```python
import functools
import math
import jax
import jax.numpy as jnp
from jax import lax
from jax.experimental import pallas as pl
from jax.experimental.pallas import tpu as pltpu
from jax.sharding import PartitionSpec as P

LN_EPS = 1e-5
KEY_TILE = 256
Q_BLOCK = 256
FOLD = 16
AUG = 96
VMEM_BYTES = 67043328
BF = jnp.bfloat16
F32 = jnp.float32


def dot_nn(lhs, rhs):
    return lax.dot_general(lhs, rhs, (((1,), (0,)), ((), ())), preferred_element_type=F32)


def dot_nt(lhs, rhs):
    return lax.dot_general(lhs, rhs, (((1,), (1,)), ((), ())), preferred_element_type=F32)


def dot_tn(lhs, rhs):
    return lax.dot_general(lhs, rhs, (((0,), (0,)), ((), ())), preferred_element_type=F32)


def split_parts(value):
    high = value.astype(BF)
    rest = value - high.astype(F32)
    mid = rest.astype(BF)
    return high, mid, (rest - mid.astype(F32)).astype(BF)


def fold_rows(value, op):
    groups = value.reshape(value.shape[0] // FOLD, FOLD, value.shape[1])
    out = groups[0]
    for i in range(1, groups.shape[0]):
        out = op(out, groups[i])
    return out


MESH = pl.DeviceIdType.MESH
RING = 4
ROUNDS = 5
ROUND_ROWS = 256
STAGES = 8
SPARE = ((0, 1), (1, 1), (2, 1), (3, 1), (0, 6), (1, 5), (1, 6), (2, 6), (2, 6))
PIECES = 4
SENDS = 16
CUTS = 4
ORDER = ('yx', 'yy', 'yy', 'yx', 'yx')


class Links:
    def __init__(self, depth):
        dp, self.x = lax.axis_index('dp'), lax.axis_index('cp')
        self.core = lax.rem(dp, 2)
        self.y = lax.rem(dp // 2, RING)
        self.z = dp // (2 * RING)
        self.depth = depth
        self.pos = {'x': self.x, 'y': self.y, 'z': self.z}
        self.size = {'x': RING, 'y': RING, 'z': depth}
        self.peer = self.at(core=1 - self.core)
        pair, odd = self.x // 2, lax.rem(self.x, 2)
        self.owners = [(pair, 2 * self.core + odd), (pair, 2 * self.core + 1 - odd)]
        self.workers = [(pair, 2 * self.core), (pair, 2 * self.core + 1)]

    def at(self, x=None, y=None, z=None, core=None):
        pick = lambda value, own: own if value is None else value
        return ((pick(z, self.z) * RING + pick(y, self.y)) * 2 + pick(core, self.core), pick(x, self.x))

    def step(self, axis, d):
        return self.at(**{axis: lax.rem(self.pos[axis] + d, self.size[axis])})

    def is_self(self, place):
        return jnp.logical_and(place[0] == self.core, place[1] == self.x)


def remote(source, target, send, recv, device):
    return pltpu.make_async_remote_copy(src_ref=source, dst_ref=target, send_sem=send, recv_sem=recv,
                                        device_id=device, device_id_type=MESH)


def wait_for(ref, sem):
    pltpu.make_async_copy(ref, ref, sem).wait()


class GradReduce:
    def __init__(self, links, dim, grad, out, results, bufs, sems):
        self.links, self.grad, self.both, self.out = links, grad, out, out.at[links.core]
        width = grad.shape[0] // 4
        self.pieces = [(0, width, results[0], 0)]
        self.pieces += [(width + (3 * head + k) * dim, dim, results[1 + k], head * dim) for head in range(width // dim) for k in range(3)]
        self.recv1, self.recv2, self.mid, self.z_src, self.z_recv, self.z_out = bufs
        self.rs_sems, self.ag_sems, self.z_sems, self.swap_sems, self.store_sems = sems

    def axes(self, rnd, unit):
        first = ORDER[rnd][unit]
        return first, ('x' if first == 'y' else 'y')

    def block(self, rnd, unit, phase):
        first = rnd * ROUND_ROWS + unit * 128
        if phase == 0:
            return first, 32
        return first + self.links.pos[self.axes(rnd, unit)[0]] * 32, 8

    def landing(self, rnd, unit, phase):
        return (self.recv1 if phase == 0 else self.recv2).at[rnd, unit]

    def wait_all(self, rnd, unit, phase, sems):
        whole = self.landing(rnd, unit, phase)
        every = remote(whole, whole, sems.at[0, rnd, unit, phase], sems.at[1, rnd, unit, phase], self.links.peer)
        every.wait_recv()
        every.wait_send()

    def source(self, rnd, unit, phase, owner):
        if phase == 0:
            first, rows = self.block(rnd, unit, 0)
            return self.grad.at[pl.ds(pl.multiple_of(first + owner * rows, 8), rows)]
        return self.mid.at[rnd, unit, pl.ds(pl.multiple_of(owner * 8, 8), 8)]

    def scatter_start(self, rnd, unit, phase):
        axis = self.axes(rnd, unit)[phase]
        for d in (2, 1, 3):
            owner = lax.rem(self.links.pos[axis] + d, RING)
            remote(self.source(rnd, unit, phase, owner), self.landing(rnd, unit, phase).at[d - 1],
                   self.rs_sems.at[0, rnd, unit, phase], self.rs_sems.at[1, rnd, unit, phase], self.links.step(axis, d)).start()

    def scatter_end(self, rnd, unit, phase):
        self.wait_all(rnd, unit, phase, self.rs_sems)
        landing = self.landing(rnd, unit, phase)
        mine = self.source(rnd, unit, phase, self.links.pos[self.axes(rnd, unit)[phase]])
        return (mine[...] + landing[0]) + (landing[1] + landing[2])

    def gather_start(self, rnd, unit, phase):
        axis = self.axes(rnd, unit)[phase]
        first, rows = self.block(rnd, unit, phase)
        part = self.out.at[pl.ds(pl.multiple_of(first + self.links.pos[axis] * rows, 8), rows)]
        for d in (2, 1, 3):
            remote(part, part, self.ag_sems.at[0, rnd, unit, phase], self.ag_sems.at[1, rnd, unit, phase],
                   self.links.step(axis, d)).start()

    def z_copies(self, rnd, way):
        links = self.links
        each = 16 // links.depth
        send, recv = self.z_sems.at[0, rnd, way], self.z_sems.at[1, rnd, way]
        mine = pl.ds(links.z * each, each)
        copies = []
        for d in range(1, links.depth):
            far = lax.rem(links.z + d, links.depth)
            if way == 0:
                source, target = self.z_src.at[rnd, pl.ds(far * each, each)], self.z_recv.at[rnd, d - 1]
            else:
                source = target = self.z_out.at[rnd, mine]
            copies.append(remote(source, target, send, recv, links.step('z', d)))
        return copies, mine

    def z_wait(self, rnd, way):
        if self.links.depth > 1:
            whole = self.z_recv.at[rnd]
            all_of = remote(whole, whole, self.z_sems.at[0, rnd, way], self.z_sems.at[1, rnd, way], self.links.step('z', 1))
            all_of.wait_recv()
            all_of.wait_send()

    def swap(self, rnd):
        part = self.out.at[pl.ds(rnd * ROUND_ROWS, ROUND_ROWS)]
        return remote(part, part, self.swap_sems.at[0, rnd], self.swap_sems.at[1, rnd], self.links.peer)

    def store(self, rnd):
        begin = rnd * ROUND_ROWS
        half = self.both.shape[1] // 4
        for first, rows, result, place in self.pieces:
            low, high = max(first, begin), min(first + rows, begin + ROUND_ROWS)
            for core in range(2):
                if low < high:
                    target = result.at[pl.ds(core * half + place + low - first, high - low)]
                    pltpu.make_async_copy(self.both.at[core, pl.ds(low, high - low)], target, self.store_sems.at[rnd]).start()

    def stored(self, rnd):
        wait_for(self.both.at[:, pl.ds(rnd * ROUND_ROWS, ROUND_ROWS)], self.store_sems.at[rnd])

    def stage(self, rnd, k):
        units = (0, 1)
        if k == 0:
            for u in units:
                self.scatter_start(rnd, u, 0)
        elif k == 1:
            for u in units:
                self.mid[rnd, u] = self.scatter_end(rnd, u, 0)
                self.scatter_start(rnd, u, 1)
        elif k == 2:
            for u in units:
                total = self.scatter_end(rnd, u, 1)
                for j in range(5):
                    self.z_src[rnd, u * 5 + j] = total[:, j * 128:(j + 1) * 128]
            self.z_src[rnd, pl.ds(10, 6)] = jnp.zeros((6, 8, 128), F32)
            for copy in self.z_copies(rnd, 0)[0]:
                copy.start()
        elif k == 3:
            self.z_wait(rnd, 0)
            copies, mine = self.z_copies(rnd, 1)
            total = self.z_src[rnd, mine]
            for d in range(self.links.depth - 1):
                total = total + self.z_recv[rnd, d]
            self.z_out[rnd, mine] = total
            for copy in copies:
                copy.start()
        elif k == 4:
            self.z_wait(rnd, 1)
            for u in units:
                first = self.block(rnd, u, 1)[0] + self.links.pos[self.axes(rnd, u)[1]] * 8
                for j in range(5):
                    self.out[pl.ds(pl.multiple_of(first, 8), 8), pl.ds(j * 128, 128)] = self.z_out[rnd, u * 5 + j]
                self.gather_start(rnd, u, 1)
        elif k == 5:
            for u in units:
                self.wait_all(rnd, u, 1, self.ag_sems)
                self.gather_start(rnd, u, 0)
        elif k == 6:
            for u in units:
                self.wait_all(rnd, u, 0, self.ag_sems)
            self.swap(rnd).start()
        else:
            self.swap(rnd).wait()
            self.store(rnd)


def layer_norm(x_ref, rows):
    x_f = x_ref[rows].astype(F32)
    centered = x_f - jnp.mean(x_f, axis=-1, keepdims=True)
    inv_std = lax.rsqrt(jnp.mean(centered * centered, axis=-1, keepdims=True) + LN_EPS)
    return centered * inv_std, inv_std


def padded(parts, rows):
    filled = [part.astype(F32) for part in parts]
    used = sum(part.shape[0] for part in filled)
    return jnp.concatenate(filled + [jnp.zeros((rows - used, filled[0].shape[1]), F32)], axis=0).astype(BF)


def block_body(dim, depth, x_hbm, dy_hbm, wq_hbm, wk_hbm, wv_hbm, wo_hbm, gamma_ref, beta_ref, bo_ref,
               y_ref, gx_ref, dq_ref, dk_ref, dv_ref, dwo_ref, small_ref,
               x_s, normed_s, dy_s, wt_s, wo_s, q_s, k_s, v_s, do_s, o_s, of_s, o_peer, lse_s, kf_s, vf_s, buf_a, buf_b, buf_c,
               kb_s, vb_s, dk_acc, dv_acc, grads, grads_peer, d_w, d_w_all, dx_s, y_s,
               recv1, recv2, mid, z_src, z_recv, z_out, small_s, small_recv,
               load_sems, in_send, in_recv, pass_send, pass_recv, o_sems, grad_sems, out_send, out_recv, small_sems,
               rs_sems, ag_sems, z_sems, swap_sems, store_sems):
    links = Links(depth)
    width, tokens = q_s.shape
    heads, tiles = width // dim, tokens // KEY_TILE
    own, band = tokens // 2, tokens // 4
    scale = dim ** -0.5
    log2_scale = scale * math.log2(math.e)
    fwd_group, bwd_group = tiles, 4
    fwd_steps, bwd_steps = tiles // fwd_group, tiles // bwd_group
    zero = jnp.minimum(links.x, 0)
    gamma, beta, bias = (ref[...].reshape(1, ref.shape[0]) for ref in (gamma_ref, beta_ref, bo_ref))
    odd = lax.rem(links.x, 2)
    reduce = GradReduce(links, dim, d_w, d_w_all, (dwo_ref, dq_ref, dk_ref, dv_ref), (recv1, recv2, mid, z_src, z_recv, z_out),
                        (rs_sems, ag_sems, z_sems, swap_sems, store_sems))
    end = heads * bwd_steps + 1
    plan = {}
    for rnd in range(ROUNDS):
        at = rnd * bwd_steps + 1 if rnd else 0
        for k in range(STAGES):
            at += min(k, 1) + SPARE.count((rnd, k))
            plan.setdefault(at, []).append((rnd, k))
    for at in plan:
        plan[at].sort(key=lambda item: (item[1] in (0, 5) and item[0] < ROUNDS - 1, -item[0]))
    slots = max(plan) + 1 - end

    def tile_rows(tile, base=None):
        return pl.ds(tile * KEY_TILE if base is None else pl.multiple_of(base + tile * KEY_TILE, KEY_TILE), KEY_TILE)

    def head_rows(head, rows=dim):
        return pl.ds(pl.multiple_of(head * rows, 16), rows)

    def q_cols(index):
        return pl.ds(pl.multiple_of(index * Q_BLOCK, Q_BLOCK), Q_BLOCK)

    def my_half(side):
        return pl.ds(pl.multiple_of((links.core if side == 0 else 1 - links.core) * width, 16), width)

    loads = [pltpu.make_async_copy(w_hbm.at[my_half(side)], wt_s.at[side, pl.ds(k * width, width)], load_sems.at[side, k])
             for side in range(2) for k, w_hbm in enumerate((wq_hbm, wk_hbm, wv_hbm))]
    loads += [pltpu.make_async_copy(wo_hbm.at[my_half(side)], wo_s.at[side], load_sems.at[side, 3]) for side in range(2)]

    def maybe_far(place, source, target, send, recv):
        core, x = place
        here = links.is_self(place)
        far = remote(source, target, send, recv, links.at(core=core, x=x))
        near = pltpu.make_async_copy(source, target, recv)

        @pl.when(jnp.logical_not(here))
        def _():
            far.start()

        @pl.when(here)
        def _():
            near.start()

    def all_left(ref, sem):
        rows = ref.shape[0]
        halved = links.x // 2 == links.core

        @pl.when(jnp.logical_not(halved))
        def _():
            wait_for(ref, sem)

        @pl.when(halved)
        def _():
            wait_for(ref.at[pl.ds(0, rows // 2)], sem)

    piece = band // PIECES

    def deliver(which, m, c):
        slot = lax.rem(links.x + m, 2)
        source = (dy_hbm if which else x_hbm).at[m, pl.ds(c * piece, piece)]
        target = (dy_s if which else x_s).at[pl.ds(pl.multiple_of(slot * band + c * piece, 16), piece)]
        maybe_far(links.workers[m], source, target, in_send.at[which], in_recv.at[which, slot, c])

    def hand_over(which, slot, c):
        rows = dy_s if which else x_s
        first = slot * band + c * piece
        return remote(rows.at[pl.ds(first, piece)], rows.at[pl.ds(own + first, piece)],
                      pass_send.at[which], pass_recv.at[which, slot, c], links.peer)

    def arrive(which, slot, c):
        wait_for((dy_s if which else x_s).at[pl.ds(slot * band + c * piece, piece)], in_recv.at[which, slot, c])
        hand_over(which, slot, c).start()

    def swap_out(head):
        rows = head_rows(head)
        return remote(o_s.at[rows, pl.ds(own, own)], o_peer.at[rows], o_sems.at[0, head], o_sems.at[1, head], links.peer)

    def swap_grads(head):
        rows = head_rows(head)
        return remote(grads.at[:, rows, pl.ds(own, own)], grads_peer.at[:, rows], grad_sems.at[0, head], grad_sems.at[1, head],
                      links.peer)

    part = band // 2
    portion = own // SENDS

    def send_home(which, i):
        cut = SENDS // 2
        second, inner = i // cut, lax.rem(i, cut)
        source = (dx_s if which else y_s).at[pl.ds(pl.multiple_of(i * portion, 16), portion)]
        target = (gx_ref if which else y_ref).at[odd, pl.ds(pl.multiple_of(inner * portion, 16), portion)]
        (core, x0), (_, x1) = links.owners
        maybe_far((core, jnp.where(second == 0, x0, x1)), source, target, out_send.at[which], out_recv.at[which])

    barrier = pltpu.get_barrier_semaphore()
    fixed = [links.peer]
    fixed += [links.step(axis, d) for axis in ('x', 'y') for d in range(1, RING)]
    fixed += [links.step('z', d) for d in range(1, depth)]
    for device in fixed:
        pl.semaphore_signal(barrier, inc=1, device_id=device, device_id_type=MESH)
    count = len(fixed)
    for place in links.owners + links.workers:
        other = jnp.logical_not(links.is_self(place))
        count = count + other.astype(jnp.int32)

        @pl.when(other)
        def _():
            pl.semaphore_signal(barrier, inc=1, device_id=links.at(core=place[0], x=place[1]), device_id_type=MESH)
    for load in loads:
        load.start()
    pl.semaphore_wait(barrier, count)
    for c in range(PIECES):
        for m in range(2):
            deliver(0, m, c)
    for load in loads:
        load.wait()

    def normalize(first):
        rows = pl.ds(first, piece)
        normed_s[rows] = (layer_norm(x_s, rows)[0] * gamma + beta).astype(BF)

    def project(b, c):
        cols = pl.ds(b * band + (c - 2) * piece, 2 * piece)
        normed = normed_s[cols]
        for k, out in enumerate((q_s, k_s, v_s)):
            out[:, cols] = dot_nt(wt_s[0, pl.ds(k * width, width)], normed).astype(BF)

    for c in range(PIECES + 1):
        if c < PIECES:
            for slot in range(2):
                arrive(0, slot, c)
            if c == PIECES - 1:
                for i in range(PIECES):
                    for m in range(2):
                        deliver(1, m, i)
            for slot in range(2):
                normalize(slot * band + c * piece)
        if c:
            if c % 2 == 0:
                project(0, c)
                project(1, c)
            for slot in range(2):
                hand_over(0, slot, c - 1).wait_recv()
                normalize(own + slot * band + (c - 1) * piece)
                if c % 2 == 0:
                    project(2 + slot, c)

    def forward_step(now, carry):
        head, step = now // fwd_steps, lax.rem(now, fwd_steps)
        rows = head_rows(head)
        for c in range(PIECES):
            @pl.when(now == max(c, 1))
            def _():
                for slot in range(2):
                    arrive(1, slot, c)

        @pl.when(step == 0)
        def _():
            k_t = k_s[rows]
            kf_s[...] = jnp.concatenate([k_t, k_t, k_t], axis=0).T
            vf_s[0:dim] = v_s[rows]
            vf_s[dim:] = padded([jnp.ones((1, tokens), F32)], AUG - dim)

        bufs = (buf_a, buf_b, buf_c)
        total, lag = tiles * fwd_group, tiles + 2
        query, high, top, probs, out = {}, {}, {}, {}, {}
        for g in range(total + lag + 2):
            if g < total:
                i, t = divmod(g, tiles)
                if t == 0:
                    query[i] = jnp.concatenate(split_parts(q_s[rows, q_cols(step * fwd_group + i)].astype(F32) * log2_scale), axis=0)
                scores = dot_nn(kf_s[tile_rows(t)], query[i])
                bufs[i % 3][tile_rows(t)] = scores
                folded = fold_rows(scores, jnp.maximum)
                high[i] = folded if t == 0 else jnp.maximum(high[i], folded)
                if t == tiles - 1:
                    top[i] = jnp.max(high[i], axis=0, keepdims=True)
            if lag <= g < total + lag:
                i, t = divmod(g - lag, tiles)
                probs[g - lag] = jnp.exp2(bufs[i % 3][tile_rows(t, zero)] - top[i]).astype(BF)
            if g >= lag + 2:
                i, t = divmod(g - lag - 2, tiles)
                product = dot_nn(vf_s[:, tile_rows(t)], probs[g - lag - 2])
                out[i] = product if t == 0 else out[i] + product
                if t == tiles - 1:
                    cols = q_cols(step * fwd_group + i)
                    denom = out[i][dim:dim + 1]
                    value = out[i][:dim] * (1.0 / denom)
                    o_s[rows, cols] = value.astype(BF)
                    of_s[rows, cols] = value
                    lse = (top[i] + jnp.log2(denom)) * (1.0 / log2_scale)
                    lse_s[head_rows(head, 16), cols] = padded(split_parts(lse), 16)

        @pl.when(step == fwd_steps - 1)
        def _():
            swap_out(head).start()

        return carry

    lax.fori_loop(0, heads * fwd_steps, forward_step, 0)
    for c in range(PIECES):
        for slot in range(2):
            hand_over(1, slot, c).wait_recv()
    d_w[pl.ds(0, width)] = dot_nn(o_s[...], dy_s[...])
    for rnd, k in plan[0]:
        reduce.stage(rnd, k)
    for i in range(tiles):
        cols = pl.ds(i * KEY_TILE, KEY_TILE)
        do_s[:, cols] = dot_nt(wo_s[0], dy_s[cols]).astype(BF)
    for head in range(heads):
        swap_out(head).wait()
    for i in range(4):
        toks = pl.ds(i * part, part)
        product = dot_tn(o_s[:, toks], wo_s[0]) + dot_tn(o_peer[:, toks], wo_s[1])
        y_s[toks] = (x_s[toks].astype(F32) + product + bias).astype(BF)
    for which in range(2):
        rows = (dy_s if which else x_s).at[pl.ds(0, own)]
        all_left(rows, in_send.at[which])
        wait_for(rows, pass_send.at[which])

    def backward_step(now, carry):
        head, step = now // bwd_steps, lax.rem(now, bwd_steps)
        rows = head_rows(head)
        for at in range(end - 1):
            todo = plan.get(at + 1)
            if todo:
                @pl.when(now == at)
                def _():
                    for rnd, k in todo:
                        reduce.stage(rnd, k)
        share = SENDS // (heads * bwd_steps)
        for i in range(share):
            send_home(0, now * share + i)

        @pl.when(step == 0)
        def _():
            minus = padded([jnp.full((3, tokens), -1.0, F32)], AUG - dim)
            kb_s[...] = jnp.concatenate([k_s[rows], minus], axis=0).T
            vb_s[...] = jnp.concatenate([v_s[rows], minus], axis=0).T
            dk_acc[...] = jnp.zeros_like(dk_acc)
            dv_acc[...] = jnp.zeros_like(dv_acc)

        total = tiles * bwd_group
        ops, probs, d_scores, dq = {}, {}, {}, {}
        for g in range(total + 2):
            if g < total:
                i, t = divmod(g, tiles)
                if t == 0:
                    cols = q_cols(step * bwd_group + i)
                    q_t, do_t = q_s[rows, cols], do_s[rows, cols]
                    delta = jnp.sum(of_s[rows, cols] * do_t.astype(F32), axis=0, keepdims=True)
                    ops[i] = (cols, q_t, do_t, jnp.concatenate([q_t, lse_s[head_rows(head, 16), cols]], axis=0),
                              jnp.concatenate([do_t, padded(split_parts(delta), 16)], axis=0))
                scores = dot_nn(kb_s[tile_rows(t)], ops[i][3])
                d_probs = dot_nn(vb_s[tile_rows(t)], ops[i][4])
                prob = jnp.exp2(scores * log2_scale)
                probs[g] = prob.astype(BF)
                d_scores[g] = (prob * d_probs).astype(BF)
            if g >= 2:
                i, t = divmod(g - 2, tiles)
                cols, q_t, do_t = ops[i][:3]
                dv_acc[:, tile_rows(t)] += dot_nt(do_t, probs[g - 2])
                product = dot_nn(k_s[rows, tile_rows(t)], d_scores[g - 2])
                dq[i] = product if t == 0 else dq[i] + product
                if t == tiles - 1:
                    grads[0, rows, cols] = (dq[i] * scale).astype(BF)
                dk_acc[:, tile_rows(t)] += dot_nt(q_t, d_scores[g - 2])

        @pl.when(step == bwd_steps - 1)
        def _():
            grads[1, rows] = (dk_acc[...] * scale).astype(BF)
            grads[2, rows] = dv_acc[...].astype(BF)
            swap_grads(head).start()
            stacked = jnp.concatenate([grads[0, rows], grads[1, rows], grads[2, rows]], axis=0)
            d_w[pl.ds(pl.multiple_of(width + head * (3 * dim), 8), 3 * dim)] = dot_nn(stacked, normed_s[...])

        return carry

    lax.fori_loop(0, heads * bwd_steps, backward_step, 0)

    def tail(slot):
        for rnd, k in plan.get(end + slot, ()):
            reduce.stage(rnd, k)

    tail(0)
    for head in range(heads):
        swap_grads(head).wait()
    sums = [jnp.zeros((1, 640), F32)] * 3
    for i in range(4):
        toks = pl.ds(i * part, part)
        mine = jnp.concatenate([grads[k, :, toks] for k in range(3)], axis=0)
        theirs = jnp.concatenate([grads_peer[k, :, toks] for k in range(3)], axis=0)
        d_normed = (dot_tn(mine, wt_s[0]) + dot_tn(theirs, wt_s[1])).astype(BF).astype(F32)
        x_hat, inv_std = layer_norm(x_s, toks)
        d_hat = d_normed * gamma
        mean_one = jnp.mean(d_hat, axis=-1, keepdims=True)
        mean_two = jnp.mean(d_hat * x_hat, axis=-1, keepdims=True)
        dy_f = dy_s[toks].astype(F32)
        dx_s[toks] = (dy_f + inv_std * (d_hat - mean_one - x_hat * mean_two)).astype(BF)
        for k, term in enumerate((d_normed * x_hat, d_normed, dy_f)):
            sums[k] = sums[k] + jnp.sum(term, axis=0, keepdims=True)

    for k in range(3):
        for j in range(5):
            small_s[0, pl.ds(k * 5 + j, 1)] = sums[k][:, j * 128:(j + 1) * 128]
    small_s[0, pl.ds(15, 1)] = jnp.zeros((1, 128), F32)
    small_copy = pltpu.make_async_copy(small_s.at[4], small_ref, load_sems.at[0, 0])
    first, waiting = 0, ()
    for hop, axis in enumerate(('z', 'core', 'y', 'x', '')):
        if hop:
            for slot in range(hop, hop + 1 if axis else slots):
                tail(slot)
            if hop == 1:
                for i in range(SENDS):
                    send_home(1, i)
            acc = small_s[hop - 1]
            for d, copy in enumerate(waiting):
                copy.wait_recv()
                acc = acc + small_recv[first + d]
            for copy in waiting:
                copy.wait_send()
            first += len(waiting)
            small_s[hop] = acc
        if axis:
            far = [links.peer] if axis == 'core' else [links.step(axis, d) for d in range(1, links.size[axis])]
            waiting = [remote(small_s.at[hop], small_recv.at[first + d], small_sems.at[0, first + d], small_sems.at[1, first + d],
                              device) for d, device in enumerate(far)]
            for copy in waiting:
                copy.start()
    small_copy.start()
    for which in range(2):
        all_left(dx_s if which else y_s, out_send.at[which])
        wait_for(gx_ref if which else y_ref, out_recv.at[which])
    for rnd in range(ROUNDS):
        reduce.stored(rnd)
    small_copy.wait()


def attention_block(x_in, grad_y, weights, vectors, dim, depth):
    rows, channels = x_in.shape[1:]
    tokens, own = 4 * rows, 2 * rows
    width = weights[0].shape[0] // 2
    heads = width // dim
    total = 4 * width
    half = lambda *shape: pltpu.VMEM(shape, BF)
    full = lambda *shape: pltpu.VMEM(shape, F32)
    dma = lambda *shape: pltpu.SemaphoreType.DMA(shape)
    anywhere = pl.BlockSpec(memory_space=pl.ANY)
    in_vmem = pl.BlockSpec(memory_space=pltpu.VMEM)
    far = max(depth - 1, 1)
    return pl.pallas_call(
        functools.partial(block_body, dim, depth),
        in_specs=[anywhere] * 6 + [in_vmem] * 3,
        out_specs=[anywhere] * 7,
        out_shape=[jax.ShapeDtypeStruct(x_in.shape, BF)] * 2
        + [jax.ShapeDtypeStruct(weights[0].shape, F32)] * 4 + [jax.ShapeDtypeStruct((16, 128), F32)],
        scratch_shapes=[half(tokens, channels)] * 3 + [half(2, 3 * width, channels), half(2, width, channels)]
        + [half(width, tokens)] * 5 + [full(width, tokens), half(width, own), half(16 * heads, tokens),
                                       half(tokens, 3 * dim), half(AUG, tokens)]
        + [full(tokens, Q_BLOCK)] * 3 + [half(tokens, AUG)] * 2 + [full(dim, tokens)] * 2
        + [half(3, width, tokens), half(3, width, own), full(total, channels), full(2, total, channels)]
        + [half(own, channels)] * 2
        + [full(ROUNDS, 2, 3, 32, channels), full(ROUNDS, 2, 3, 8, channels), full(ROUNDS, 2, 32, channels), full(ROUNDS, 16, 8, 128),
           full(ROUNDS, far, 16 // depth, 8, 128), full(ROUNDS, 16, 8, 128), full(5, 16, 128), full(7 + far, 16, 128),
           dma(2, 4)] + [dma(2), dma(2, 2, PIECES)] * 2 + [dma(2, heads)] * 2
        + [dma(2), dma(2), dma(2, 7 + far)] + [dma(2, ROUNDS, 2, 2)] * 2 + [dma(2, ROUNDS, 2), dma(2, ROUNDS), dma(ROUNDS)],
        compiler_params=pltpu.CompilerParams(collective_id=0, has_side_effects=True, vmem_limit_bytes=VMEM_BYTES),
        name='attention_block',
    )(x_in, grad_y, *weights, *vectors)


def settle_body(count, small_hbm, *refs):
    sources, targets, refs = refs[:count], refs[count:2 * count], refs[2 * count:]
    vectors, bufs, (small, vector_s, sems, vector_sems) = refs[:3], refs[3:3 + count], refs[3 + count:]
    load = pltpu.make_async_copy(small_hbm, small, vector_sems.at[3])
    load.start()
    cuts = []
    for i, (source, target, buf) in enumerate(zip(sources, targets, bufs)):
        rows = source.shape[0] // CUTS
        for c in range(CUTS):
            part = pl.ds(c * rows, rows)
            cuts.append((pltpu.make_async_copy(source.at[part], buf.at[part], sems.at[0, i, c]),
                         pltpu.make_async_copy(buf.at[part], target.at[part], sems.at[1, i, c])))
    for read, _ in cuts:
        read.start()
    load.wait()
    stores = []
    for k, vector in enumerate(vectors):
        vector_s[k][...] = jnp.concatenate([small[k * 5 + j:k * 5 + j + 1] for j in range(5)], axis=1).reshape(vector.shape)
        stores.append(pltpu.make_async_copy(vector_s[k], vector, vector_sems.at[k]))
        stores[k].start()
    for read, write in cuts:
        read.wait()
        write.start()
    for _, write in cuts:
        write.wait()
    for store in stores:
        store.wait()


def settle(small, arrays):
    anywhere = pl.BlockSpec(memory_space=pl.ANY)
    count = len(arrays)
    dma = pltpu.SemaphoreType.DMA
    vector = (arrays[0].shape[1],)
    return pl.pallas_call(
        functools.partial(settle_body, count),
        in_specs=[anywhere] * (count + 1), out_specs=[anywhere] * (count + 3),
        out_shape=[jax.ShapeDtypeStruct(a.shape, a.dtype) for a in arrays] + [jax.ShapeDtypeStruct(vector, F32)] * 3,
        scratch_shapes=[pltpu.VMEM(a.shape, a.dtype) for a in arrays]
        + [pltpu.VMEM(small.shape, F32), [pltpu.VMEM(vector, F32)] * 3, dma((2, count, CUTS)), dma((4,))],
        compiler_params=pltpu.CompilerParams(vmem_limit_bytes=VMEM_BYTES),
        name='settle',
    )(small, *arrays)


def solution(mesh):
    depth = mesh.shape['dp'] // (2 * RING)
    act_spec, rep_spec = P('dp', 'cp', None), P()

    def device_step(x_in, grad_y, ln_gamma, ln_beta, w_q, w_k, w_v, w_o, b_o):
        channels, num_heads, head_dim = w_q.shape
        flat = (num_heads * head_dim, channels)
        weights = [jnp.transpose(w, (1, 2, 0)).reshape(flat) for w in (w_q, w_k, w_v)] + [w_o.reshape(flat)]
        y_out, grad_x, *grads, grad_wo, small = attention_block(x_in, grad_y, weights, (ln_gamma, ln_beta, b_o), head_dim, depth)
        rows = (2 * y_out.shape[1], channels)
        moved = settle(small, [y_out.reshape(rows), grad_x.reshape(rows), *grads, grad_wo])
        y_out, grad_x = (a.reshape(x_in.shape) for a in moved[:2])
        grads, grad_wo = moved[2:5], moved[5]
        grads = [jnp.transpose(grad.reshape(num_heads, head_dim, channels), (2, 0, 1)) for grad in grads]
        return (y_out, grad_x, moved[6], moved[7], *grads, grad_wo.reshape(num_heads, head_dim, channels), moved[8])

    specs = (act_spec, act_spec) + (rep_spec,) * 7
    return jax.shard_map(device_step, mesh=mesh, in_specs=specs, out_specs=specs, check_vma=False)
```

profile of v0, /device:TPU:1, one launch (start us, length us, event | category | flops | bytes accessed | tf_op | source)
XLA Modules:
  0.0 143.9 jit_solution(13525989659067765528)
XLA Ops:
  0.6 135.8 %attention_block.1 = (bf16[2,512,640]{2,1,0:T(8,128)(2,1)}, bf16[2,512,640]{2,1,0:T(8,128)(2,1)}, f32[640,640]{1,0:T(8,128)}, f32[640,640]{1,0:T(8,128)}, f32[64...) custom-call(bf16[2,512,640]{2,1,0:T(8,128)(2,1)} %x_hbm.1, bf16[2,512,640]{2,1,0:T(8,128)(2,1)} %dy_hbm.1, ...), custom_call_target="tpu_custom_call" | custom-call | tf_op jit(solution)/shard_map/attention_block/pallas_call | solution.py:613
  136.5 7.3 %settle.1 = (bf16[1024,640]{1,0:T(8,128)(2,1)}, bf16[1024,640]{1,0:T(8,128)(2,1)}, f32[640,640]{1,0:T(8,128)}, f32[640,640]{1,0:T(8,128)}, f32[640,640]{1,0:T(8,...) custom-call(f32[16,128]{1,0:T(8,128)} %get-tuple-element.25.small_hbm, ...), custom_call_target="tpu_custom_call" | custom-call | tf_op jit(solution)/shard_map/settle/pallas_call | solution.py:668
where the time goes:
time: 144 us
  Pallas kernels  143 us (99%)
    pallas_call x1, Pallas kernels, attention_block(): pl.pallas_call(functools.partial(block_body, dim, depth), in_specs=[anywh...  136 us
    pallas_call x1, Pallas kernels, settle(): pl.pallas_call(functools.partial(settle_body, count), in_specs=[anywhere]...  7.27 us

commit v1 on v0

--- a/solution.py
+++ b/solution.py
@@ -49,10 +49,10 @@
 ROUNDS = 5
 ROUND_ROWS = 256
 STAGES = 8
-SPARE = ((0, 1), (1, 1), (2, 1), (3, 1), (0, 6), (1, 5), (1, 6), (2, 6), (2, 6))
+SPARE = ((0, 1), (0, 2), (1, 1), (2, 1), (3, 1), (0, 6), (1, 5), (1, 6), (2, 6), (2, 6))
 PIECES = 4
 SENDS = 16
-CUTS = 4
+CUTS = 8
 ORDER = ('yx', 'yy', 'yy', 'yx', 'yx')
 
 

time: 144 us -> 146 us (1.014)
  Pallas kernels: 143 us -> 145 us
    pallas_call x1, Pallas kernels: 136 us -> 138 us  [attention_block(): pl.pallas_call(functools.partial(block_body, dim, depth), in_specs=[anywh...]
where the time goes in v1:
time: 146 us
  Pallas kernels  145 us (99%)
    pallas_call x1, Pallas kernels, attention_block(): pl.pallas_call(functools.partial(block_body, dim, depth), in_specs=[anywh...  138 us
    pallas_call x1, Pallas kernels, settle(): pl.pallas_call(functools.partial(settle_body, count), in_specs=[anywhere]...  7.86 us

profile of v1, /device:TPU:1, one launch (start us, length us, event | category | flops | bytes accessed | tf_op | source)
XLA Modules:
  0.0 146.3 jit_solution(5021859248788412547)
XLA Ops:
  0.6 137.6 %attention_block.1 = (bf16[2,512,640]{2,1,0:T(8,128)(2,1)}, bf16[2,512,640]{2,1,0:T(8,128)(2,1)}, f32[640,640]{1,0:T(8,128)}, f32[640,640]{1,0:T(8,128)}, f32[64...) custom-call(bf16[2,512,640]{2,1,0:T(8,128)(2,1)} %x_hbm.1, bf16[2,512,640]{2,1,0:T(8,128)(2,1)} %dy_hbm.1, ...), custom_call_target="tpu_custom_call" | custom-call | tf_op jit(solution)/shard_map/attention_block/pallas_call | solution.py:613
  138.2 7.9 %settle.1 = (bf16[1024,640]{1,0:T(8,128)(2,1)}, bf16[1024,640]{1,0:T(8,128)(2,1)}, f32[640,640]{1,0:T(8,128)}, f32[640,640]{1,0:T(8,128)}, f32[640,640]{1,0:T(8,...) custom-call(f32[16,128]{1,0:T(8,128)} %get-tuple-element.25.small_hbm, ...), custom_call_target="tpu_custom_call" | custom-call | tf_op jit(solution)/shard_map/settle/pallas_call | solution.py:668
